TPU v7x, 32 devices: a whole 2x2x4 slice. The times are simulated.
32 devices in a mesh: ep: 4 (over y, x), fsdp: 8 (over z, core).
Axes of the slice: x: 2, y: 2, z: 4, core: 2. Of those that a mesh axis runs over, the one named last changes fastest.
Arguments:
- w_gate: float32 [64, 2048, 1024], P('ep', 'fsdp'), may hold values from -0.1875 to 0.1875
- avg_gate: bfloat16 [64, 2048, 1024], P('ep', 'fsdp'), may hold values from -0.0625 to 0.0625
- w_up: float32 [64, 2048, 1024], P('ep', 'fsdp'), may hold values from -0.1875 to 0.1875
- avg_up: bfloat16 [64, 2048, 1024], P('ep', 'fsdp'), may hold values from -0.0625 to 0.0625
- w_down: float32 [64, 1024, 2048], P('ep', None, 'fsdp'), may hold values from -0.25 to 0.25
- avg_down: bfloat16 [64, 1024, 2048], P('ep', None, 'fsdp'), may hold values from -0.09375 to 0.09375
- router_weight: float32 [2048, 64], P('fsdp', 'ep'), may hold values from -0.125 to 0.125
- router_gain: float32 [2048], P('fsdp'), may hold values from 0.25 to 1.75
Outputs:
- serve_gate: bfloat16 [64, 2048, 1024], P('ep', None, 'fsdp')
- serve_up: bfloat16 [64, 2048, 1024], P('ep', None, 'fsdp')
- serve_down: bfloat16 [64, 1024, 2048], P('ep', 'fsdp')
- scale_gate: float32 [64, 1024], P('ep', 'fsdp')
- scale_up: float32 [64, 1024], P('ep', 'fsdp')
- scale_down: float32 [64, 1024], P('ep', 'fsdp')
- serve_router: bfloat16 [2048, 64], replicated
All inputs are finite; a program needn't handle non-finite values.
Results may differ from a plain program's by a relative error of at most 0.001.
Values may be sent and summed in bfloat16 or wider, within the bound.
A program may use at most 192 MiB of HBM per device.

v0:
```python
import jax
import jax.numpy as jnp
from jax import lax
from jax.sharding import PartitionSpec as P


def on_device(w_gate, avg_gate, w_up, avg_up, w_down, avg_down, router_weight, router_gain):
    fresh_gate = w_gate + avg_gate.astype(jnp.float32)
    fresh_up = w_up + avg_up.astype(jnp.float32)
    fresh_down = w_down + avg_down.astype(jnp.float32)
    total_gate, total_up, total_down = lax.psum(
        (
            jnp.sum(fresh_gate * fresh_gate, axis=1),
            jnp.sum(fresh_up * fresh_up, axis=1),
            jnp.sum(fresh_down * fresh_down, axis=2),
        ),
        "fsdp",
    )
    scale_gate = jnp.sqrt(total_gate)
    scale_up = jnp.sqrt(total_up)
    scale_down = jnp.sqrt(total_down)
    narrow_gate, narrow_up, narrow_down = (
        (fresh_gate / jnp.expand_dims(scale_gate, 1)).astype(jnp.bfloat16),
        (fresh_up / jnp.expand_dims(scale_up, 1)).astype(jnp.bfloat16),
        (fresh_down / jnp.expand_dims(scale_down, 2)).astype(jnp.bfloat16),
    )
    serve_gate, serve_up = (
        lax.all_to_all(narrow_gate, "fsdp", split_axis=2, concat_axis=1, tiled=True),
        lax.all_to_all(narrow_up, "fsdp", split_axis=2, concat_axis=1, tiled=True),
    )
    serve_down = lax.all_to_all(narrow_down, "fsdp", split_axis=1, concat_axis=2, tiled=True)
    scale_gate = lax.dynamic_slice_in_dim(
        scale_gate, lax.axis_index("fsdp") * serve_gate.shape[2], serve_gate.shape[2], axis=1
    )
    scale_up = lax.dynamic_slice_in_dim(
        scale_up, lax.axis_index("fsdp") * serve_up.shape[2], serve_up.shape[2], axis=1
    )
    scale_down = lax.dynamic_slice_in_dim(
        scale_down, lax.axis_index("fsdp") * serve_down.shape[1], serve_down.shape[1], axis=1
    )
    part_router = (router_weight * router_gain[:, None]).astype(jnp.bfloat16)
    row_router = lax.all_gather(part_router, "fsdp", axis=0, tiled=True)
    serve_router = lax.all_gather(row_router, "ep", axis=1, tiled=True)
    return (serve_gate, serve_up, serve_down, scale_gate, scale_up, scale_down, serve_router)


def solution(mesh):
    placed = (
        P("ep", "fsdp", None),
        P("ep", "fsdp", None),
        P("ep", "fsdp", None),
        P("ep", "fsdp", None),
        P("ep", None, "fsdp"),
        P("ep", None, "fsdp"),
        P("fsdp", "ep"),
        P("fsdp"),
    )
    return jax.shard_map(
        on_device,
        mesh=mesh,
        in_specs=placed,
        out_specs=(
            P("ep", None, "fsdp"),
            P("ep", None, "fsdp"),
            P("ep", "fsdp", None),
            P("ep", "fsdp"),
            P("ep", "fsdp"),
            P("ep", "fsdp"),
            P(),
        ),
        check_vma=False,
    )
```

profile of v0, /device:TPU:0, one launch (start us, length us, event | category | flops | bytes accessed | tf_op | source)
XLA Modules:
  0.0 824.8 jit_solution(4685212397091970850)
XLA Ops:
  7.2 0.0 all-reduce.3.cloned.1.call-start
  7.2 17.6 %copy.31 = f32[16,256,1024]{1,0,2:T(8,128)} copy(f32[16,256,1024]{2,1,0:T(8,128)} %param.8) | data formatting | bytes 33554432 | tf_op args[0]
  24.8 17.6 %copy.34 = f32[16,256,1024]{1,0,2:T(8,128)} copy(f32[16,256,1024]{2,1,0:T(8,128)} %param.10) | data formatting | bytes 33554432 | tf_op args[2]
  42.4 12.5 %copy.30 = bf16[16,256,1024]{1,0,2:T(8,128)(2,1)} copy(bf16[16,256,1024]{2,1,0:T(8,128)(2,1)} %param.9) | data formatting | bytes 16777216 | tf_op args[1]
  54.9 12.5 %copy.33 = bf16[16,256,1024]{1,0,2:T(8,128)(2,1)} copy(bf16[16,256,1024]{2,1,0:T(8,128)(2,1)} %param.11) | data formatting | bytes 16777216 | tf_op args[3]
  67.4 25.2 %multiply_reduce_fusion = f32[16,1024]{0,1:T(8,128)} fusion(f32[16,1024,256]{2,1,0:T(8,128)} %param.12, bf16[16,1024,256]{2,1,0:T(8,128)(2,1)} %param.13), kind=kLoop, calls=%fused_computation.2 | loop fusion | flops 16760832 | bytes 25231360 | tf_op jit(solution)/shard_map/reduce_sum | solution.py:15
  92.6 13.2 %multiply_reduce_fusion.1 = (f32[16,1024]{0,1:T(8,128)}, f32[16,1024]{0,1:T(8,128)}) fusion(f32[16,256,1024]{1,0,2:T(8,128)} %copy.34, bf16[16,256,1024]{1,0,2:T(8,128)(2,1)S(1)} %copy-done.1, f32[16,256,1024]{1,0,2:T(8,128)} %copy.31, bf16[16,256,1024]{1,0,2:T(8,128)(2,1)S(1)} %copy-done), kind=kLoop, calls=%fused_computation.4 | loop fusion | flops 33521664 | bytes 50462720 | tf_op jit(solution)/shard_map/reduce_sum | solution.py:14
  105.8 0.0 all-reduce.3.cloned.1.call-update
  105.8 65.1 %all-reduce.3.cloned.1.call-done = (f32[16,1024]{0,1:T(8,128)}, f32[16,1024]{0,1:T(8,128)}, f32[16,1024]{0,1:T(8,128)}) async-done(((f32[16,1024]{0,1:T(8,128)}, f32[16,1024]{0,1:T(8,128)}, f32[16,1024]{0,1:T(8,128)}), (f32[16,1024]{0,1:T(8,128)}, f32[16,1024]{0,1:T(8,128)}, f32[16,1024]{0,1:T(8,128)})) %all-reduce.3.cloned.1.call-update) | async-done | bytes 196624 | tf_op jit(solution)/shard_map/psum | solution.py:11
  170.9 1.2 sqrt.10
  172.1 12.0 %divide_convert_fusion.1 = bf16[16,256,1024]{1,0,2:T(8,128)(2,1)} fusion(f32[16,256,1024]{1,0,2:T(8,128)} %copy.34, bf16[16,256,1024]{1,0,2:T(8,128)(2,1)} %copy.33, f32[16,1024]{0,1:T(8,128)S(1)} %sqrt.10), kind=kLoop, calls=%fused_computation.3 | loop fusion | flops 16777216 | bytes 33619968 | tf_op jit(solution)/shard_map/convert_element_type | solution.py:24
  184.1 5.1 all-to-all-start.1
  189.2 0.1 sqrt.9
  189.3 12.0 %divide_convert_fusion.2 = bf16[16,256,1024]{1,0,2:T(8,128)(2,1)} fusion(f32[16,256,1024]{1,0,2:T(8,128)} %copy.31, bf16[16,256,1024]{1,0,2:T(8,128)(2,1)} %copy.30, f32[16,1024]{0,1:T(8,128)S(1)} %sqrt.9), kind=kLoop, calls=%fused_computation.6 | loop fusion | flops 16777216 | bytes 33619968 | tf_op jit(solution)/shard_map/convert_element_type | solution.py:23
  201.3 171.7 %all-to-all-done.1 = bf16[16,256,1024]{1,0,2:T(8,128)(2,1)} async-done(((bf16[16,256,1024]{1,0,2:T(8,128)(2,1)}), bf16[16,256,1024]{1,0,2:T(8,128)(2,1)}, u32[]{:S(2)}, u32[]{:S(2)}) %all-to-all-start.1) | async-done | bytes 8388640 | tf_op jit(solution)/shard_map/all_to_all | solution.py:29
  373.0 5.1 all-to-all-start
  378.2 0.1 sqrt.11
  378.3 23.8 %divide_convert_fusion = bf16[16,1024,256]{2,0,1:T(8,128)(2,1)} fusion(f32[16,1024,256]{2,1,0:T(8,128)} %param.12, f32[16,1024]{0,1:T(8,128)S(1)} %sqrt.11, bf16[16,1024,256]{2,1,0:T(8,128)(2,1)} %param.13), kind=kLoop, calls=%fused_computation.1 | loop fusion | flops 16777216 | bytes 33619968 | tf_op jit(solution)/shard_map/convert_element_type | solution.py:25
  402.1 159.8 %all-to-all-done = bf16[16,256,1024]{1,0,2:T(8,128)(2,1)} async-done(((bf16[16,256,1024]{1,0,2:T(8,128)(2,1)}), bf16[16,256,1024]{1,0,2:T(8,128)(2,1)}, u32[]{:S(2)}, u32[]{:S(2)}) %all-to-all-start) | async-done | bytes 8388640 | tf_op jit(solution)/shard_map/all_to_all | solution.py:28
  561.8 5.0 all-to-all-start.2
  566.9 0.0 copy-done.4
  566.9 189.9 %all_gather.6 = bf16[2048,16]{0,1:T(8,128)(2,1)S(1)} all-gather(bf16[256,16]{0,1:T(8,128)(2,1)S(1)} %multiply_convert_fusion), channel_id=1, replica_groups=mesh['ep'=4,'fsdp'=8] {'fsdp'}, dimensions={0}, use_global_device_ids=true | all-gather | bytes 73728 | tf_op jit(solution)/shard_map/all_gather | solution.py:42
  756.8 9.1 %all_gather.7 = bf16[2048,64]{0,1:T(8,128)(2,1)S(1)} all-gather(bf16[2048,16]{0,1:T(8,128)(2,1)S(1)} %all_gather.6), channel_id=1, replica_groups=mesh['ep'=4,'fsdp'=8] {'ep'}, dimensions={1}, use_global_device_ids=true | all-gather | bytes 327680 | tf_op jit(solution)/shard_map/all_gather | solution.py:43
  765.9 0.7 copy.39
  766.6 0.7 copy.40
  767.3 0.7 copy.41
  767.9 12.3 %copy.35 = bf16[16,8,256,128]{3,2,1,0:T(8,128)(2,1)} copy(bf16[16,8,256,128]{2,0,3,1:T(8,128)(2,1)} %bitcast.4) | data formatting | bytes 16777216 | tf_op jit(solution)/shard_map/all_to_all | solution.py:29
  780.2 12.3 %copy.32 = bf16[16,8,256,128]{3,2,1,0:T(8,128)(2,1)} copy(bf16[16,8,256,128]{2,0,3,1:T(8,128)(2,1)} %bitcast.1) | data formatting | bytes 16777216 | tf_op jit(solution)/shard_map/all_to_all | solution.py:28
  792.5 0.0 all-to-all-done.2
  792.5 11.4 %copy.38 = bf16[16,128,8,256]{3,2,1,0:T(8,128)(2,1)} copy(bf16[16,128,8,256]{3,0,1,2:T(8,128)(2,1)} %bitcast.7) | data formatting | bytes 16777216 | tf_op jit(solution)/shard_map/all_to_all | solution.py:31
  803.9 13.4 %all_to_all.50 = bf16[16,128,2048]{2,1,0:T(8,128)(2,1)} reshape(bf16[16,128,8,256]{3,2,1,0:T(8,128)(2,1)} %copy.38) | data formatting | bytes 16777216 | tf_op jit(solution)/shard_map/all_to_all | solution.py:31
  817.3 0.7 copy.53
  (15 shorter events, 0.0 us)
Async XLA Ops:
  7.2 163.7 %all-reduce.3.cloned.1.call-start = ((), (), s32[]{:S(2)}) async-start(), calls=%async_computation.3 | async-start | bytes 3145728 | tf_op jit(solution)/shard_map/psum | solution.py:11
  67.4 25.2 %copy-start = (bf16[16,256,1024]{1,0,2:T(8,128)(2,1)S(1)}, bf16[16,256,1024]{1,0,2:T(8,128)(2,1)}, u32[]{:S(2)}) copy-start(bf16[16,256,1024]{1,0,2:T(8,128)(2,1)} %copy.30) | copy-start | bytes 25165828
  67.4 25.2 %copy-start.1 = (bf16[16,256,1024]{1,0,2:T(8,128)(2,1)S(1)}, bf16[16,256,1024]{1,0,2:T(8,128)(2,1)}, u32[]{:S(2)}) copy-start(bf16[16,256,1024]{1,0,2:T(8,128)(2,1)} %copy.33) | copy-start | bytes 25165828
  184.1 5.1 copy-start.3
  184.1 189.0 %all-to-all-start.1 = ((bf16[16,256,1024]{1,0,2:T(8,128)(2,1)}), bf16[16,256,1024]{1,0,2:T(8,128)(2,1)}, u32[]{:S(2)}, u32[]{:S(2)}) async-start(bf16[16,256,1024]{1,0,2:T(8,128)(2,1)} %divide_convert_fusion.1), calls=%async_computation.1 | async-start | bytes 16777216 | tf_op jit(solution)/shard_map/all_to_all | solution.py:29
  201.3 176.9 %copy-start.2 = (f32[16,1024]{0,1:T(8,128)S(1)}, f32[16,1024]{0,1:T(8,128)}, u32[]{:S(2)}) copy-start(f32[16,1024]{0,1:T(8,128)} %get-tuple-element.16) | copy-start | bytes 196612
  373.0 188.8 %all-to-all-start = ((bf16[16,256,1024]{1,0,2:T(8,128)(2,1)}), bf16[16,256,1024]{1,0,2:T(8,128)(2,1)}, u32[]{:S(2)}, u32[]{:S(2)}) async-start(bf16[16,256,1024]{1,0,2:T(8,128)(2,1)} %divide_convert_fusion.2), calls=%async_computation | async-start | bytes 16777216 | tf_op jit(solution)/shard_map/all_to_all | solution.py:28
  402.1 164.8 %copy-start.4 = (f32[256,16]{0,1:T(8,128)S(1)}, f32[256,16]{0,1:T(8,128)}, u32[]{:S(2)}) copy-start(f32[256,16]{0,1:T(8,128)} %param.14) | copy-start | bytes 49156
  402.1 164.8 %copy-start.5 = (f32[256]{0:T(256)S(1)}, f32[256]{0:T(256)}, u32[]{:S(2)}) copy-start(f32[256]{0:T(256)} %param.15) | copy-start | bytes 3076
  561.8 230.7 %all-to-all-start.2 = ((bf16[16,1024,256]{2,0,1:T(8,128)(2,1)}), bf16[16,1024,256]{2,0,1:T(8,128)(2,1)}, u32[]{:S(2)}, u32[]{:S(2)}) async-start(bf16[16,1024,256]{2,0,1:T(8,128)(2,1)} %divide_convert_fusion), calls=%async_computation.2 | async-start | bytes 16777216 | tf_op jit(solution)/shard_map/all_to_all | solution.py:31
Sparse Core Ops, SparseCore 0:
  105.9 64.9 all-reduce.2
where the time goes:
time: 827 us; the launch traced here: 825 us
  waiting for transfers between devices  397 us (48%)
  blocking collectives  199 us (24%)
  local copies, waits for them, and re-layouts  114 us (14%)
  other arithmetic  86.1 us (10%)
  starting transfers between devices  15.3 us (2%)
  between operations  14.1 us (2%)
    all_gather x1, blocking collectives, on_device(): row_router = lax.all_gather(part_router, 'fsdp', axis=0, tiled=True)  190 us
    all_to_all x1, waiting for transfers between devices, on_device(): lax.all_to_all(narrow_up, 'fsdp', split_axis=2, concat_axis=1, tiled=True)  172 us
    all_to_all x1, waiting for transfers between devices, on_device(): lax.all_to_all(narrow_gate, 'fsdp', split_axis=2, concat_axis=1, tiled=True)  160 us
    psum x1, waiting for transfers between devices, on_device(): lax.psum((jnp.sum(fresh_gate * fresh_gate, axis=1), jnp.sum(fresh_up * fr...  65.1 us
    unnamed x20, local copies, waits for them, and re-layouts  62.9 us
    reduce_sum x1, other arithmetic, on_device(): jnp.sum(fresh_down * fresh_down, axis=2)  25.2 us
    all_to_all x2, local copies, waits for them, and re-layouts, on_device(): lax.all_to_all(narrow_down, 'fsdp', split_axis=1, concat_axis=2, tiled=True)  24.8 us
    convert_element_type x1, other arithmetic, on_device(): (fresh_down / jnp.expand_dims(scale_down, 2)).astype(jnp.bfloat16)  23.8 us
  transfers between devices with their start and end apart: 4, of which 3 were waited for; matrix products, arithmetic and copies ran while one was open for 8% of the time, Pallas kernels for 0%

commit v1 on v0

--- a/solution.py
+++ b/solution.py
@@ -26,7 +26,12 @@
     )
     serve_gate, serve_up = (
         lax.all_to_all(narrow_gate, "fsdp", split_axis=2, concat_axis=1, tiled=True),
-        lax.all_to_all(narrow_up, "fsdp", split_axis=2, concat_axis=1, tiled=True),
+        jnp.concatenate(
+            lax.all_to_all(
+                jnp.stack(jnp.split(narrow_up, lax.axis_size("fsdp"), axis=2)), "fsdp", 0, 0
+            ),
+            axis=1,
+        ),
     )
     serve_down = lax.all_to_all(narrow_down, "fsdp", split_axis=1, concat_axis=2, tiled=True)
     scale_gate = lax.dynamic_slice_in_dim(

time: 827 us -> 789 us (0.954)
  local copies, waits for them, and re-layouts: 114 us -> 89 us
  waiting for transfers between devices: 397 us -> 387 us
    unnamed x20 -> x28, local copies, waits for them, and re-layouts: 62.9 us -> 40.9 us
    all_to_all x1 -> x0, local copies, waits for them, and re-layouts: 12.3 us -> none  [on_device(): lax.all_to_all(narrow_up, 'fsdp', split_axis=2, concat_axis=1, tiled=True)]
    all_to_all x1, waiting for transfers between devices: 172 us -> 160 us  [on_device(): lax.all_to_all(jnp.stack(jnp.split(narrow_up, lax.axis_size('fsdp'), axis...]
    reduce_sum x0 -> x1, other arithmetic: none -> 10.6 us  [on_device(): jnp.sum(fresh_gate * fresh_gate, axis=1)]
    reduce_sum x1, other arithmetic: 25.2 us -> 16.8 us  [on_device(): jnp.sum(fresh_down * fresh_down, axis=2)]
where the time goes in v1:
time: 789 us; the launch traced here: 788 us
  waiting for transfers between devices  387 us (49%)
  blocking collectives  199 us (25%)
  local copies, waits for them, and re-layouts  89 us (11%)
  other arithmetic  83.6 us (11%)
  starting transfers between devices  15.3 us (2%)
  between operations  14.2 us (2%)
    all_gather x1, blocking collectives, on_device(): row_router = lax.all_gather(part_router, 'fsdp', axis=0, tiled=True)  190 us
    all_to_all x1, waiting for transfers between devices, on_device(): lax.all_to_all(narrow_gate, 'fsdp', split_axis=2, concat_axis=1, tiled=True)  164 us
    all_to_all x1, waiting for transfers between devices, on_device(): lax.all_to_all(jnp.stack(jnp.split(narrow_up, lax.axis_size('fsdp'), axis...  160 us
    psum x1, waiting for transfers between devices, on_device(): lax.psum((jnp.sum(fresh_gate * fresh_gate, axis=1), jnp.sum(fresh_up * fr...  62.6 us
    unnamed x28, local copies, waits for them, and re-layouts  40.9 us
    all_to_all x2, local copies, waits for them, and re-layouts, on_device(): lax.all_to_all(narrow_down, 'fsdp', split_axis=1, concat_axis=2, tiled=True)  24.8 us
    convert_element_type x1, other arithmetic, on_device(): (fresh_down / jnp.expand_dims(scale_down, 2)).astype(jnp.bfloat16)  23.8 us
    reduce_sum x1, other arithmetic, on_device(): jnp.sum(fresh_down * fresh_down, axis=2)  16.8 us
  transfers between devices with their start and end apart: 4, of which 3 were waited for; matrix products, arithmetic and copies ran while one was open for 8% of the time, Pallas kernels for 0%

profile of v1, /device:TPU:0, one launch (start us, length us, event | category | flops | bytes accessed | tf_op | source)
XLA Modules:
  0.0 787.9 jit_solution(3974083231037796088)
XLA Ops:
  7.2 17.6 %copy.28 = f32[16,256,1024]{1,0,2:T(8,128)} copy(f32[16,256,1024]{2,1,0:T(8,128)} %param.8) | data formatting | bytes 33554432 | tf_op args[0]
  24.8 12.5 %copy.27 = bf16[16,256,1024]{1,0,2:T(8,128)(2,1)} copy(bf16[16,256,1024]{2,1,0:T(8,128)(2,1)} %param.9) | data formatting | bytes 16777216 | tf_op args[1]
  37.3 10.6 %multiply_reduce_fusion.2 = f32[16,1024]{0,1:T(8,128)} fusion(f32[16,256,1024]{1,0,2:T(8,128)} %copy.28, bf16[16,256,1024]{1,0,2:T(8,128)(2,1)} %copy.27), kind=kLoop, calls=%fused_computation.7 | loop fusion | flops 16760832 | bytes 25231360 | tf_op jit(solution)/shard_map/reduce_sum | solution.py:13
  48.0 11.0 %multiply_reduce_fusion.1 = f32[16,1024]{1,0:T(8,128)} fusion(f32[16,256,1024]{2,1,0:T(8,128)} %param.10, bf16[16,256,1024]{2,1,0:T(8,128)(2,1)} %param.11), kind=kLoop, calls=%fused_computation.4 | loop fusion | flops 16760832 | bytes 25231360 | tf_op jit(solution)/shard_map/reduce_sum | solution.py:14
  59.0 16.8 %multiply_reduce_fusion = f32[16,1024]{0,1:T(8,128)} fusion(f32[16,1024,256]{2,1,0:T(8,128)S(1)} %bitcast.44, bf16[16,1024,256]{2,1,0:T(8,128)(2,1)} %param.13), kind=kLoop, calls=%fused_computation.2 | loop fusion | flops 16760832 | bytes 25231360 | tf_op jit(solution)/shard_map/reduce_sum | solution.py:15
  75.8 62.6 %all-reduce.3.cloned.1.call-done = (f32[16,1024]{0,1:T(8,128)}, f32[16,1024]{1,0:T(8,128)}, f32[16,1024]{0,1:T(8,128)}) async-done(((f32[16,1024]{0,1:T(8,128)}, f32[16,1024]{1,0:T(8,128)}, f32[16,1024]{0,1:T(8,128)}), (f32[16,1024]{0,1:T(8,128)}, f32[16,1024]{1,0:T(8,128)}, f32[16,1024]{0,1:T(8,128)})) %all-reduce.3.cloned.1.call-update) | async-done | bytes 196624 | tf_op jit(solution)/shard_map/psum | solution.py:11
  138.4 1.2 sqrt.9
  139.6 12.0 %divide_convert_fusion.2 = bf16[16,256,1024]{1,0,2:T(8,128)(2,1)} fusion(f32[16,256,1024]{1,0,2:T(8,128)} %copy.28, bf16[16,256,1024]{1,0,2:T(8,128)(2,1)} %copy.27, f32[16,1024]{0,1:T(8,128)S(1)} %sqrt.9), kind=kLoop, calls=%fused_computation.6 | loop fusion | flops 16777216 | bytes 33619968 | tf_op jit(solution)/shard_map/convert_element_type | solution.py:23
  151.5 5.1 all-to-all-start
  156.7 9.4 %divide_convert_fusion.1 = bf16[16,256,1024]{2,1,0:T(8,128)(2,1)S(1)} fusion(f32[16,256,1024]{2,1,0:T(8,128)} %param.10, bf16[16,256,1024]{2,1,0:T(8,128)(2,1)} %param.11, f32[16,1024]{1,0:T(8,128)S(1)} %sqrt.10), kind=kLoop, calls=%fused_computation.3 | loop fusion | flops 16777216 | bytes 33619968 | tf_op jit(solution)/shard_map/convert_element_type | solution.py:24
  166.1 1.2 fusion.7
  167.3 1.2 fusion.6
  168.6 1.2 fusion.5
  169.8 1.2 fusion.4
  171.1 1.2 fusion.3
  172.3 1.2 fusion.2
  173.6 1.2 fusion.1
  174.8 1.2 fusion
  176.1 164.4 %all-to-all-done = bf16[16,256,1024]{1,0,2:T(8,128)(2,1)} async-done(((bf16[16,256,1024]{1,0,2:T(8,128)(2,1)}), bf16[16,256,1024]{1,0,2:T(8,128)(2,1)}, u32[]{:S(2)}, u32[]{:S(2)}) %all-to-all-start) | async-done | bytes 8388640 | tf_op jit(solution)/shard_map/all_to_all | solution.py:28
  340.5 5.2 all-to-all-start.1
  345.9 23.8 %divide_convert_fusion = bf16[16,1024,256]{2,0,1:T(8,128)(2,1)} fusion(f32[16,1024,256]{2,1,0:T(8,128)} %param.12, f32[16,1024]{0,1:T(8,128)S(1)} %sqrt.11, bf16[16,1024,256]{2,1,0:T(8,128)(2,1)} %param.13), kind=kLoop, calls=%fused_computation.1 | loop fusion | flops 16777216 | bytes 33619968 | tf_op jit(solution)/shard_map/convert_element_type | solution.py:25
  369.7 159.7 %all-to-all-done.1 = bf16[8,16,256,128]{3,2,1,0:T(8,128)(2,1)} async-done(((bf16[8,16,256,128]{3,2,1,0:T(8,128)(2,1)}), bf16[8,16,256,128]{3,2,1,0:T(8,128)(2,1)}, u32[]{:S(2)}, u32[]{:S(2)}) %all-to-all-start.1) | async-done | bytes 8388640 | tf_op jit(solution)/shard_map/all_to_all | solution.py:30
  529.4 5.0 all-to-all-start.2
  534.4 189.9 %all_gather.6 = bf16[2048,16]{0,1:T(8,128)(2,1)S(1)} all-gather(bf16[256,16]{0,1:T(8,128)(2,1)S(1)} %multiply_convert_fusion), channel_id=1, replica_groups=mesh['ep'=4,'fsdp'=8] {'fsdp'}, dimensions={0}, use_global_device_ids=true | all-gather | bytes 73728 | tf_op jit(solution)/shard_map/all_gather | solution.py:47
  724.3 9.1 %all_gather.7 = bf16[2048,64]{0,1:T(8,128)(2,1)S(1)} all-gather(bf16[2048,16]{0,1:T(8,128)(2,1)S(1)} %all_gather.6), channel_id=1, replica_groups=mesh['ep'=4,'fsdp'=8] {'ep'}, dimensions={1}, use_global_device_ids=true | all-gather | bytes 327680 | tf_op jit(solution)/shard_map/all_gather | solution.py:48
  733.4 0.7 copy.34
  734.1 0.7 copy.35
  735.4 12.3 %copy.29 = bf16[16,8,256,128]{3,2,1,0:T(8,128)(2,1)} copy(bf16[16,8,256,128]{2,0,3,1:T(8,128)(2,1)} %bitcast.1) | data formatting | bytes 16777216 | tf_op jit(solution)/shard_map/all_to_all | solution.py:28
  747.6 7.9 %copy.30 = bf16[16,8,256,128]{3,2,1,0:T(8,128)(2,1)} copy(bf16[16,8,256,128]{3,2,0,1:T(8,128)(2,1)} %bitcast.11) | data formatting | bytes 16777216 | tf_op jit(solution)/shard_map/reshape | solution.py:29
  755.5 11.4 %copy.33 = bf16[16,128,8,256]{3,2,1,0:T(8,128)(2,1)} copy(bf16[16,128,8,256]{3,0,1,2:T(8,128)(2,1)} %bitcast.14) | data formatting | bytes 16777216 | tf_op jit(solution)/shard_map/all_to_all | solution.py:36
  766.9 13.4 %all_to_all.37 = bf16[16,128,2048]{2,1,0:T(8,128)(2,1)} reshape(bf16[16,128,8,256]{3,2,1,0:T(8,128)(2,1)} %copy.33) | data formatting | bytes 16777216 | tf_op jit(solution)/shard_map/all_to_all | solution.py:36
  780.3 0.7 copy.54
  (25 shorter events, 0.8 us)
Async XLA Ops:
  7.2 131.2 %all-reduce.3.cloned.1.call-start = ((), (), s32[]{:S(2)}) async-start(), calls=%async_computation.3 | async-start | bytes 2228224 | tf_op jit(solution)/shard_map/psum | solution.py:11
  37.3 21.7 %slice-start = ((s8[16777216]{0:T(1024)(128)(4,1)}), s8[4194304]{0:T(1024)(128)(4,1)S(1)}, s32[]{:S(2)}) async-start(s8[16777216]{0:T(1024)(128)(4,1)} %bitcast.43), calls=%async_computation.4 | async-start | bytes 8388608
  37.3 21.7 %slice-start.1 = ((s8[16777216]{0:T(1024)(128)(4,1)}), s8[4194304]{0:T(1024)(128)(4,1)S(1)}, s32[]{:S(2)}) async-start(s8[16777216]{0:T(1024)(128)(4,1)} %bitcast.43), calls=%async_computation.5 | async-start | bytes 8388608
  37.3 21.7 %slice-start.2 = ((s8[16777216]{0:T(1024)(128)(4,1)}), s8[4194304]{0:T(1024)(128)(4,1)S(1)}, s32[]{:S(2)}) async-start(s8[16777216]{0:T(1024)(128)(4,1)} %bitcast.43), calls=%async_computation.6 | async-start | bytes 8388608
  48.0 11.0 %slice-start.3 = ((s8[16777216]{0:T(1024)(128)(4,1)}), s8[4194304]{0:T(1024)(128)(4,1)S(1)}, s32[]{:S(2)}) async-start(s8[16777216]{0:T(1024)(128)(4,1)} %bitcast.43), calls=%async_computation.7 | async-start | bytes 8388608
  151.5 5.1 copy-start.1
  151.5 188.9 %all-to-all-start = ((bf16[16,256,1024]{1,0,2:T(8,128)(2,1)}), bf16[16,256,1024]{1,0,2:T(8,128)(2,1)}, u32[]{:S(2)}, u32[]{:S(2)}) async-start(bf16[16,256,1024]{1,0,2:T(8,128)(2,1)} %divide_convert_fusion.2), calls=%async_computation | async-start | bytes 16777216 | tf_op jit(solution)/shard_map/all_to_all | solution.py:28
  176.1 169.7 %copy-start = (f32[16,1024]{0,1:T(8,128)S(1)}, f32[16,1024]{0,1:T(8,128)}, u32[]{:S(2)}) copy-start(f32[16,1024]{0,1:T(8,128)} %get-tuple-element.16) | copy-start | bytes 196612
  340.5 188.9 %all-to-all-start.1 = ((bf16[8,16,256,128]{3,2,1,0:T(8,128)(2,1)}), bf16[8,16,256,128]{3,2,1,0:T(8,128)(2,1)}, u32[]{:S(2)}, u32[]{:S(2)}) async-start(bf16[8,16,256,128]{3,2,1,0:T(8,128)(2,1)} %fusion), calls=%async_computation.1 | async-start | bytes 16777216 | tf_op jit(solution)/shard_map/all_to_all | solution.py:30
  369.6 164.7 %copy-start.2 = (f32[256,16]{0,1:T(8,128)S(1)}, f32[256,16]{0,1:T(8,128)}, u32[]{:S(2)}) copy-start(f32[256,16]{0,1:T(8,128)} %param.14) | copy-start | bytes 49156
  369.6 164.7 %copy-start.3 = (f32[256]{0:T(256)S(1)}, f32[256]{0:T(256)}, u32[]{:S(2)}) copy-start(f32[256]{0:T(256)} %param.15) | copy-start | bytes 3076
  529.4 226.1 %all-to-all-start.2 = ((bf16[16,1024,256]{2,0,1:T(8,128)(2,1)}), bf16[16,1024,256]{2,0,1:T(8,128)(2,1)}, u32[]{:S(2)}, u32[]{:S(2)}) async-start(bf16[16,1024,256]{2,0,1:T(8,128)(2,1)} %divide_convert_fusion), calls=%async_computation.2 | async-start | bytes 16777216 | tf_op jit(solution)/shard_map/all_to_all | solution.py:36
Sparse Core Ops, SparseCore 0:
  75.9 62.4 all-reduce.2
